TPU v7x, 32 devices: a whole 2x2x4 slice. The times are simulated.
32 devices in a mesh: gx: 2 (over y), gy: 4 (over x, core), gz: 4 (over z).
Axes of the slice: x: 2, y: 2, z: 4, core: 2. Of those that a mesh axis runs over, the one named last changes fastest.
Arguments:
- loads: float32 [16, 4, 16, 1024], P(None, 'gx', 'gy', 'gz'), may hold values from -60 to 60
- moduli: float32 [8], replicated, may hold values from 0.5 to 4
- material: int32 [4, 16, 1024], P('gx', 'gy', 'gz'), may hold values from 0 to 7
Outputs:
- solution: float32 [16, 4, 16, 1024], P(None, 'gx', 'gy', 'gz')
- residual: float32 [16, 4, 16, 1024], P(None, 'gx', 'gy', 'gz')
All inputs are finite; a program needn't handle non-finite values.
Results may differ from a plain program's by a relative error of at most 0.005.
The roundings to bfloat16 on the way count: a program that leaves them out, or rounds other values in their place, can miss the bound.
Values may be sent and summed in bfloat16 or wider, within the bound.
A program may use at most 64 MiB of HBM per device.

v0:
```python
import jax
import jax.numpy as jnp
import numpy as np
from jax import lax
from jax.sharding import PartitionSpec as P

ITERS = 2
SIGMA = 0.25


def padded_2(cells, sides, width):
    for axis, dim in sides:
        count = lax.axis_size(axis)
        ends = count - 1
        head = lax.slice_in_dim(cells, 0, width, axis=dim)
        tail = lax.slice_in_dim(cells, cells.shape[dim] - width, cells.shape[dim], axis=dim)
        cells = jnp.concatenate(
            [
                lax.ppermute(tail, axis, [(i, (i + 1) % count) for i in range(ends)]),
                cells,
                lax.ppermute(head, axis, [((i + 1) % count, i) for i in range(ends)]),
            ],
            axis=dim,
        )
    return cells


def stiffness_table():
    line_mass = np.array([[1.0 / 3.0, 1.0 / 6.0], [1.0 / 6.0, 1.0 / 3.0]])
    line_stiff = np.array([[1.0, -1.0], [-1.0, 1.0]])
    table = np.zeros((8, 8))
    for target in range(8):
        for source in range(8):
            target_bits = [target >> 2 & 1, target >> 1 & 1, target & 1]
            source_bits = [source >> 2 & 1, source >> 1 & 1, source & 1]
            total = 0.0
            for stiff_dim in range(3):
                factor = 1.0
                for other in range(3):
                    if other == stiff_dim:
                        factor = factor * line_stiff[target_bits[other], source_bits[other]]
                    else:
                        factor = factor * line_mass[target_bits[other], source_bits[other]]
                total = total + factor
            table[target, source] = total
    return table


def corner_bits(corner):
    return (corner >> 2 & 1, corner >> 1 & 1, corner & 1)


def apply_operator(field, weights, kernel):
    lowered = field.astype(jnp.bfloat16)
    padded = padded_2(lowered, (("gx", 1), ("gy", 2), ("gz", 3)), 1)
    size_x, size_y, size_z = (field.shape[1], field.shape[2], field.shape[3])
    pieces = []
    for corner in range(8):
        bit_x, bit_y, bit_z = corner_bits(corner)
        pieces.append(
            padded[
                :,
                bit_x : bit_x + size_x + 1,
                bit_y : bit_y + size_y + 1,
                bit_z : bit_z + size_z + 1,
            ]
        )
    stacked = jnp.stack(pieces)
    total = SIGMA * field
    for corner in range(8):
        bit_x, bit_y, bit_z = corner_bits(corner)
        part = (
            jnp.einsum("b,bcxyz->cxyz", kernel[corner], stacked, preferred_element_type=jnp.float32)
            * weights
        )
        total = (
            total
            + part[
                :,
                1 - bit_x : 1 - bit_x + size_x,
                1 - bit_y : 1 - bit_y + size_y,
                1 - bit_z : 1 - bit_z + size_z,
            ]
        )
    return total


def local_gram(left, right):
    return jnp.einsum("cxyz,dxyz->cd", left, right, precision=lax.Precision.HIGHEST)


def combine(block, coeffs):
    return jnp.einsum("cxyz,cd->dxyz", block, coeffs, precision=lax.Precision.HIGHEST)


def solve_small(matrix, rhs_small):
    factor = jnp.linalg.cholesky(matrix)
    return jax.scipy.linalg.cho_solve((factor, True), rhs_small)


def residual_gram(residual):
    return lax.psum(local_gram(residual, residual), ("gx", "gy", "gz"))


def on_device(loads, moduli, material):
    kernel = jnp.asarray(stiffness_table(), jnp.float32).astype(jnp.bfloat16)
    levels = jnp.arange(moduli.shape[0], dtype=jnp.int32)
    node_modulus = jnp.sum(jnp.where(material[..., None] == levels, moduli, 0.0), axis=-1)
    padded_mod = padded_2(node_modulus, (("gx", 0), ("gy", 1), ("gz", 2)), 1)
    size_x, size_y, size_z = material.shape
    weights = jnp.zeros((size_x + 1, size_y + 1, size_z + 1), jnp.float32)
    for corner in range(8):
        bit_x, bit_y, bit_z = corner_bits(corner)
        weights = (
            weights
            + padded_mod[
                bit_x : bit_x + size_x + 1, bit_y : bit_y + size_y + 1, bit_z : bit_z + size_z + 1
            ]
        )
    weights = weights * 0.125
    solution = jnp.zeros_like(loads)
    residual = loads
    direction = loads
    current = residual_gram(residual)
    for iteration in range(ITERS):
        image = apply_operator(direction, weights, kernel)
        curvature, cross, image_sq = lax.psum(
            (local_gram(direction, image), local_gram(image, residual), local_gram(image, image)),
            ("gx", "gy", "gz"),
        )
        alpha = solve_small(curvature, current)
        solution = solution + combine(direction, alpha)
        residual = residual - combine(image, alpha)
        if iteration + 1 < ITERS:
            high = lax.Precision.HIGHEST
            cross_term = jnp.dot(alpha.T, cross, precision=high)
            quad_term = jnp.dot(jnp.dot(alpha.T, image_sq, precision=high), alpha, precision=high)
            updated = current - cross_term - cross_term.T + quad_term
            beta = solve_small(current, updated)
            direction = residual + combine(direction, beta)
            current = updated
    return (solution, residual)


def solution(mesh):
    in_specs = (P(None, "gx", "gy", "gz"), P(), P("gx", "gy", "gz"))
    out_specs = (P(None, "gx", "gy", "gz"), P(None, "gx", "gy", "gz"))
    return jax.shard_map(
        on_device, mesh=mesh, in_specs=in_specs, out_specs=out_specs, check_vma=False
    )
```

profile of v0, /device:TPU:0, one launch (start us, length us, event | category | flops | bytes accessed | tf_op | source)
XLA Modules:
  0.0 185.7 jit_solution(12359744168205889732)
XLA Ops:
  0.6 0.8 select_reduce_fusion
  1.4 4.9 %collective-permute-start.6 = (f32[1,4,256]{2,1,0:T(4,128)S(1)}, f32[1,4,256]{2,1,0:T(4,128)S(1)}, u32[]{:S(2)}, u32[]{:S(2)}) collective-permute-start(f32[1,4,256]{2,1,0:T(4,128)S(1)} %get-tuple-element.42), channel_id=1, source_target_pairs={{0,16},{1,17},{2,18},{3,19},{4,20},{5,21},{6,22},{7,23},{8,24},{9,... | collective-permute-start | bytes 12296 | tf_op jit(solution)/shard_map/ppermute | solution.py:19
  6.4 1.3 collective-permute-start.7
  7.7 0.9 convert_element_type.9
  8.6 4.5 %collective-permute-start = (bf16[16,1,4,256]{3,2,1,0:T(4,128)(2,1)S(1)}, bf16[16,1,4,256]{3,2,1,0:T(4,128)(2,1)S(1)}, u32[]{:S(2)}, u32[]{:S(2)}) collective-permute-start(bf16[16,1,4,256]{3,2,1,0:T(4,128)(2,1)S(1)} %get-tuple-element.26), channel_id=1, source_target_pairs={{0,16},{1,17},{2,18},{3,19},{4,20},{5,21},{6,22},{7,23},{8,24},{9,... | collective-permute-start | bytes 98312 | tf_op jit(solution)/shard_map/ppermute | solution.py:19
  13.2 1.3 collective-permute-start.1
  14.5 1.3 collective-permute-start.8
  15.8 1.3 collective-permute-start.9
  17.1 1.3 convolution_bitcast_fusion.4
  18.4 2.2 %collective-permute-done.9 = f32[4,1,256]{2,1,0:T(1,128)S(1)} collective-permute-done((f32[4,1,256]{2,1,0:T(1,128)S(1)}, f32[4,1,256]{2,1,0:T(1,128)S(1)}, u32[]{:S(2)}, u32[]{:S(2)}) %collective-permute-start.9) | collective-permute-done | bytes 4128 | tf_op jit(solution)/shard_map/ppermute | solution.py:21
  20.7 3.5 %collective-permute-start.10 = (f32[4,6,1]{2,1,0:T(8,128)S(1)}, f32[4,6,1]{2,1,0:T(8,128)S(1)}, u32[]{:S(2)}, u32[]{:S(2)}) collective-permute-start(f32[4,6,1]{2,1,0:T(8,128)S(1)} %get-tuple-element.36), channel_id=1, source_target_pairs={{0,1},{1,2},{2,3},{4,5},{5,6},{6,7},{8,9},{9,10},{10,11},{12,13},{... | collective-permute-start | bytes 296 | tf_op jit(solution)/shard_map/ppermute | solution.py:19
  24.2 1.3 collective-permute-start.11
  25.6 4.2 %collective-permute-done.11 = f32[4,6,1]{2,1,0:T(8,128)S(1)} collective-permute-done((f32[4,6,1]{2,1,0:T(8,128)S(1)}, f32[4,6,1]{2,1,0:T(8,128)S(1)}, u32[]{:S(2)}, u32[]{:S(2)}) %collective-permute-start.11) | collective-permute-done | bytes 128 | tf_op jit(solution)/shard_map/ppermute | solution.py:21
  30.1 2.8 %collective-permute-start.2 = (bf16[16,4,1,256]{3,2,1,0:T(2,128)(2,1)S(1)}, bf16[16,4,1,256]{3,2,1,0:T(2,128)(2,1)S(1)}, u32[]{:S(2)}, u32[]{:S(2)}) collective-permute-start(bf16[16,4,1,256]{3,2,1,0:T(2,128)(2,1)S(1)} %get-tuple-element.22), channel_id=1, source_target_pairs={{0,4},{4,8},{8,12},{1,5},{5,9},{9,13},{2,6},{6,10},{10,14},{3,7},{... | collective-permute-start | bytes 98312 | tf_op jit(solution)/shard_map/ppermute | solution.py:19
  33.0 1.3 collective-permute-start.3
  34.3 2.8 %collective-permute-done.3 = bf16[16,4,1,256]{3,2,1,0:T(2,128)(2,1)S(1)} collective-permute-done((bf16[16,4,1,256]{3,2,1,0:T(2,128)(2,1)S(1)}, bf16[16,4,1,256]{3,2,1,0:T(2,128)(2,1)S(1)}, u32[]{:S(2)}, u32[]{:S(2)}) %collective-permute-start.3) | collective-permute-done | bytes 32800 | tf_op jit(solution)/shard_map/ppermute | solution.py:21
  37.5 3.5 %collective-permute-start.4 = (bf16[16,4,6,1]{3,2,1,0:T(8,128)(2,1)S(1)}, bf16[16,4,6,1]{3,2,1,0:T(8,128)(2,1)S(1)}, u32[]{:S(2)}, u32[]{:S(2)}) collective-permute-start(bf16[16,4,6,1]{3,2,1,0:T(8,128)(2,1)S(1)} %get-tuple-element.15), channel_id=1, source_target_pairs={{0,1},{1,2},{2,3},{4,5},{5,6},{6,7},{8,9},{9,10},{10,11},{12,13},{... | collective-permute-start | bytes 2312 | tf_op jit(solution)/shard_map/ppermute | solution.py:19
  41.0 1.3 collective-permute-start.5
  42.4 1.1 collective-permute-done.4
  43.5 4.4 %collective-permute-done.5 = bf16[16,4,6,1]{3,2,1,0:T(8,128)(2,1)S(1)} collective-permute-done((bf16[16,4,6,1]{3,2,1,0:T(8,128)(2,1)S(1)}, bf16[16,4,6,1]{3,2,1,0:T(8,128)(2,1)S(1)}, u32[]{:S(2)}, u32[]{:S(2)}) %collective-permute-start.5) | collective-permute-done | bytes 800 | tf_op jit(solution)/shard_map/ppermute | solution.py:21
  47.8 0.9 pad_maximum_fusion
  49.3 1.6 copy.46
  51.0 0.5 fusion.82
  51.6 0.5 fusion.83
  52.2 0.5 fusion.84
  52.7 0.5 fusion.85
  53.3 0.5 fusion.86
  53.8 0.5 fusion.87
  54.4 0.5 fusion.88
  54.9 0.5 fusion.89
  55.7 0.8 copy-done
  57.3 43.2 %all-reduce = (f32[16,16]{0,1:T(8,128)S(1)}, f32[16,16]{0,1:T(8,128)S(1)}, f32[16,16]{1,0:T(8,128)S(1)}, f32[16,16]{1,0:T(8,128)S(1)}) all-reduce(f32[16,16]{0,1:T(8,128)S(1)} %convolution_bitcast_fusion.4, f32[16,16]{0,1:T(8,128)S(1)} %bitcast.265, ...), channel_id=1, replica_groups=mesh['gx'=2,'gy'=4,'gz'=4] {'gx','gy','gz'}, use_global_device_ids=true, to_apply=%region_4.0 | all-reduce | flops 1024 | bytes 8192 | tf_op jit(solution)/shard_map/psum | solution.py:102
  100.6 1.5 cholesky.70
  102.1 0.6 compare_reduce_fusion.1
  102.8 0.6 fusion.56
  103.4 1.2 custom-call.10
  104.7 1.5 cholesky.59
  106.2 0.6 compare_reduce_fusion.2
  106.9 0.6 fusion.55
  107.5 1.2 custom-call.9
  110.8 4.2 %collective-permute-start.12 = (bf16[16,1,4,256]{3,0,2,1:T(8,128)(2,1)S(1)}, bf16[16,1,4,256]{3,0,2,1:T(8,128)(2,1)S(1)}, u32[]{:S(2)}, u32[]{:S(2)}) collective-permute-start(bf16[16,1,4,256]{3,0,2,1:T(8,128)(2,1)S(1)} %get-tuple-element.24), channel_id=1, source_target_pairs={{0,16},{1,17},{2,18},{3,19},{4,20},{5,21},{6,22},{7,23},{8,24},{9,... | collective-permute-start | bytes 98312 | tf_op jit(solution)/shard_map/ppermute | solution.py:19
  115.0 1.3 collective-permute-start.13
  116.6 4.2 %collective-permute-done.13 = bf16[16,1,4,256]{3,0,2,1:T(8,128)(2,1)S(1)} collective-permute-done((bf16[16,1,4,256]{3,0,2,1:T(8,128)(2,1)S(1)}, bf16[16,1,4,256]{3,0,2,1:T(8,128)(2,1)S(1)}, u32[]{:S(2)}, u32[]{:S(2)}) %collective-permute-start.13) | collective-permute-done | bytes 32800 | tf_op jit(solution)/shard_map/ppermute | solution.py:21
  120.8 1.3 collective-permute-start.14
  122.1 1.3 collective-permute-start.15
  123.5 2.1 %collective-permute-done.15 = bf16[16,4,1,256]{3,0,2,1:T(8,128)(2,1)S(1)} collective-permute-done((bf16[16,4,1,256]{3,0,2,1:T(8,128)(2,1)S(1)}, bf16[16,4,1,256]{3,0,2,1:T(8,128)(2,1)S(1)}, u32[]{:S(2)}, u32[]{:S(2)}) %collective-permute-start.15) | collective-permute-done | bytes 32800 | tf_op jit(solution)/shard_map/ppermute | solution.py:21
  125.7 2.3 %collective-permute-start.16 = (bf16[16,4,6,1]{3,0,2,1:T(8,128)(2,1)S(1)}, bf16[16,4,6,1]{3,0,2,1:T(8,128)(2,1)S(1)}, u32[]{:S(2)}, u32[]{:S(2)}) collective-permute-start(bf16[16,4,6,1]{3,0,2,1:T(8,128)(2,1)S(1)} %get-tuple-element.19), channel_id=1, source_target_pairs={{0,1},{1,2},{2,3},{4,5},{5,6},{6,7},{8,9},{9,10},{10,11},{12,13},{... | collective-permute-start | bytes 2312 | tf_op jit(solution)/shard_map/ppermute | solution.py:19
  128.1 1.3 collective-permute-start.17
  129.7 0.6 collective-permute-done.16
  130.3 4.3 %collective-permute-done.17 = bf16[16,4,6,1]{3,0,2,1:T(8,128)(2,1)S(1)} collective-permute-done((bf16[16,4,6,1]{3,0,2,1:T(8,128)(2,1)S(1)}, bf16[16,4,6,1]{3,0,2,1:T(8,128)(2,1)S(1)}, u32[]{:S(2)}, u32[]{:S(2)}) %collective-permute-start.17) | collective-permute-done | bytes 800 | tf_op jit(solution)/shard_map/ppermute | solution.py:21
  135.1 0.5 fusion.8
  135.6 0.5 fusion.10
  136.1 0.5 fusion.12
  137.2 0.5 fusion.16
  137.7 0.5 fusion.18
  138.2 0.5 fusion.20
  138.7 0.5 fusion.22
  140.0 39.1 %psum.39 = f32[16,16]{0,1:T(8,128)S(1)} all-reduce(f32[16,16]{0,1:T(8,128)S(1)} %convolution_bitcast_fusion.1), channel_id=1, replica_groups=mesh['gx'=2,'gy'=4,'gz'=4] {'gx','gy','gz'}, use_global_device_ids=true, to_apply=%region_7.10 | all-reduce | flops 256 | bytes 2048 | tf_op jit(solution)/shard_map/psum | solution.py:127
  179.3 1.5 cholesky.81
  180.7 0.6 compare_reduce_fusion
  181.4 0.6 fusion.57
  182.0 1.2 custom-call.11
  184.0 0.7 copy.45
  185.0 0.7 copy.44
  (101 shorter events, 8.5 us)
Async XLA Ops:
  1.4 13.0 %collective-permute-start.6 = (f32[1,4,256]{2,1,0:T(4,128)S(1)}, f32[1,4,256]{2,1,0:T(4,128)S(1)}, u32[]{:S(2)}, u32[]{:S(2)}) collective-permute-start(f32[1,4,256]{2,1,0:T(4,128)S(1)} %get-tuple-element.42), channel_id=1, source_target_pairs={{0,16},{1,17},{2,18},{3,19},{4,20},{5,21},{6,22},{7,23},{8,24},{9,... | collective-permute-start | bytes 12296 | tf_op jit(solution)/shard_map/ppermute | solution.py:19
  6.4 8.1 %collective-permute-start.7 = (f32[1,4,256]{2,1,0:T(4,128)S(1)}, f32[1,4,256]{2,1,0:T(4,128)S(1)}, u32[]{:S(2)}, u32[]{:S(2)}) collective-permute-start(f32[1,4,256]{2,1,0:T(4,128)S(1)} %get-tuple-element.43), channel_id=1, source_target_pairs={{16,0},{17,1},{18,2},{19,3},{20,4},{21,5},{22,6},{23,7},{24,8},{25... | collective-permute-start | bytes 12296 | tf_op jit(solution)/shard_map/ppermute | solution.py:21
  8.6 21.3 %collective-permute-start = (bf16[16,1,4,256]{3,2,1,0:T(4,128)(2,1)S(1)}, bf16[16,1,4,256]{3,2,1,0:T(4,128)(2,1)S(1)}, u32[]{:S(2)}, u32[]{:S(2)}) collective-permute-start(bf16[16,1,4,256]{3,2,1,0:T(4,128)(2,1)S(1)} %get-tuple-element.26), channel_id=1, source_target_pairs={{0,16},{1,17},{2,18},{3,19},{4,20},{5,21},{6,22},{7,23},{8,24},{9,... | collective-permute-start | bytes 98312 | tf_op jit(solution)/shard_map/ppermute | solution.py:19
  13.2 16.8 %collective-permute-start.1 = (bf16[16,1,4,256]{3,2,1,0:T(4,128)(2,1)S(1)}, bf16[16,1,4,256]{3,2,1,0:T(4,128)(2,1)S(1)}, u32[]{:S(2)}, u32[]{:S(2)}) collective-permute-start(bf16[16,1,4,256]{3,2,1,0:T(4,128)(2,1)S(1)} %get-tuple-element.27), channel_id=1, source_target_pairs={{16,0},{17,1},{18,2},{19,3},{20,4},{21,5},{22,6},{23,7},{24,8},{25... | collective-permute-start | bytes 98312 | tf_op jit(solution)/shard_map/ppermute | solution.py:21
  14.5 3.9 %collective-permute-start.8 = (f32[4,1,256]{2,1,0:T(1,128)S(1)}, f32[4,1,256]{2,1,0:T(1,128)S(1)}, u32[]{:S(2)}, u32[]{:S(2)}) collective-permute-start(f32[4,1,256]{2,1,0:T(1,128)S(1)} %get-tuple-element.40), channel_id=1, source_target_pairs={{0,4},{4,8},{8,12},{1,5},{5,9},{9,13},{2,6},{6,10},{10,14},{3,7},{... | collective-permute-start | bytes 12296 | tf_op jit(solution)/shard_map/ppermute | solution.py:19
  15.8 4.8 %collective-permute-start.9 = (f32[4,1,256]{2,1,0:T(1,128)S(1)}, f32[4,1,256]{2,1,0:T(1,128)S(1)}, u32[]{:S(2)}, u32[]{:S(2)}) collective-permute-start(f32[4,1,256]{2,1,0:T(1,128)S(1)} %get-tuple-element.41), channel_id=1, source_target_pairs={{4,0},{8,4},{12,8},{5,1},{9,5},{13,9},{6,2},{10,6},{14,10},{7,3},{... | collective-permute-start | bytes 12296 | tf_op jit(solution)/shard_map/ppermute | solution.py:21
  20.7 4.9 %collective-permute-start.10 = (f32[4,6,1]{2,1,0:T(8,128)S(1)}, f32[4,6,1]{2,1,0:T(8,128)S(1)}, u32[]{:S(2)}, u32[]{:S(2)}) collective-permute-start(f32[4,6,1]{2,1,0:T(8,128)S(1)} %get-tuple-element.36), channel_id=1, source_target_pairs={{0,1},{1,2},{2,3},{4,5},{5,6},{6,7},{8,9},{9,10},{10,11},{12,13},{... | collective-permute-start | bytes 296 | tf_op jit(solution)/shard_map/ppermute | solution.py:19
  24.2 5.6 %collective-permute-start.11 = (f32[4,6,1]{2,1,0:T(8,128)S(1)}, f32[4,6,1]{2,1,0:T(8,128)S(1)}, u32[]{:S(2)}, u32[]{:S(2)}) collective-permute-start(f32[4,6,1]{2,1,0:T(8,128)S(1)} %get-tuple-element.37), channel_id=1, source_target_pairs={{1,0},{2,1},{3,2},{5,4},{6,5},{7,6},{9,8},{10,9},{11,10},{13,12},{... | collective-permute-start | bytes 296 | tf_op jit(solution)/shard_map/ppermute | solution.py:21
  30.1 4.2 %collective-permute-start.2 = (bf16[16,4,1,256]{3,2,1,0:T(2,128)(2,1)S(1)}, bf16[16,4,1,256]{3,2,1,0:T(2,128)(2,1)S(1)}, u32[]{:S(2)}, u32[]{:S(2)}) collective-permute-start(bf16[16,4,1,256]{3,2,1,0:T(2,128)(2,1)S(1)} %get-tuple-element.22), channel_id=1, source_target_pairs={{0,4},{4,8},{8,12},{1,5},{5,9},{9,13},{2,6},{6,10},{10,14},{3,7},{... | collective-permute-start | bytes 98312 | tf_op jit(solution)/shard_map/ppermute | solution.py:19
  33.0 4.2 %collective-permute-start.3 = (bf16[16,4,1,256]{3,2,1,0:T(2,128)(2,1)S(1)}, bf16[16,4,1,256]{3,2,1,0:T(2,128)(2,1)S(1)}, u32[]{:S(2)}, u32[]{:S(2)}) collective-permute-start(bf16[16,4,1,256]{3,2,1,0:T(2,128)(2,1)S(1)} %get-tuple-element.23), channel_id=1, source_target_pairs={{4,0},{8,4},{12,8},{5,1},{9,5},{13,9},{6,2},{10,6},{14,10},{7,3},{... | collective-permute-start | bytes 98312 | tf_op jit(solution)/shard_map/ppermute | solution.py:21
  37.5 6.0 %collective-permute-start.4 = (bf16[16,4,6,1]{3,2,1,0:T(8,128)(2,1)S(1)}, bf16[16,4,6,1]{3,2,1,0:T(8,128)(2,1)S(1)}, u32[]{:S(2)}, u32[]{:S(2)}) collective-permute-start(bf16[16,4,6,1]{3,2,1,0:T(8,128)(2,1)S(1)} %get-tuple-element.15), channel_id=1, source_target_pairs={{0,1},{1,2},{2,3},{4,5},{5,6},{6,7},{8,9},{9,10},{10,11},{12,13},{... | collective-permute-start | bytes 2312 | tf_op jit(solution)/shard_map/ppermute | solution.py:19
  41.0 6.9 %collective-permute-start.5 = (bf16[16,4,6,1]{3,2,1,0:T(8,128)(2,1)S(1)}, bf16[16,4,6,1]{3,2,1,0:T(8,128)(2,1)S(1)}, u32[]{:S(2)}, u32[]{:S(2)}) collective-permute-start(bf16[16,4,6,1]{3,2,1,0:T(8,128)(2,1)S(1)} %get-tuple-element.14), channel_id=1, source_target_pairs={{1,0},{2,1},{3,2},{5,4},{6,5},{7,6},{9,8},{10,9},{11,10},{13,12},{... | collective-permute-start | bytes 2312 | tf_op jit(solution)/shard_map/ppermute | solution.py:21
  49.3 1.6 copy-start.1
  51.0 0.7 copy-start.2
  51.0 1.2 copy-start.3
  51.6 1.1 copy-start.4
  52.2 1.1 copy-start.5
  52.7 1.1 copy-start.6
  53.3 1.1 copy-start.7
  53.8 1.1 copy-start.8
  55.6 0.9 copy-start
  110.8 5.8 %collective-permute-start.12 = (bf16[16,1,4,256]{3,0,2,1:T(8,128)(2,1)S(1)}, bf16[16,1,4,256]{3,0,2,1:T(8,128)(2,1)S(1)}, u32[]{:S(2)}, u32[]{:S(2)}) collective-permute-start(bf16[16,1,4,256]{3,0,2,1:T(8,128)(2,1)S(1)} %get-tuple-element.24), channel_id=1, source_target_pairs={{0,16},{1,17},{2,18},{3,19},{4,20},{5,21},{6,22},{7,23},{8,24},{9,... | collective-permute-start | bytes 98312 | tf_op jit(solution)/shard_map/ppermute | solution.py:19
  115.0 5.8 %collective-permute-start.13 = (bf16[16,1,4,256]{3,0,2,1:T(8,128)(2,1)S(1)}, bf16[16,1,4,256]{3,0,2,1:T(8,128)(2,1)S(1)}, u32[]{:S(2)}, u32[]{:S(2)}) collective-permute-start(bf16[16,1,4,256]{3,0,2,1:T(8,128)(2,1)S(1)} %get-tuple-element.25), channel_id=1, source_target_pairs={{16,0},{17,1},{18,2},{19,3},{20,4},{21,5},{22,6},{23,7},{24,8},{25... | collective-permute-start | bytes 98312 | tf_op jit(solution)/shard_map/ppermute | solution.py:21
  120.8 2.6 %collective-permute-start.14 = (bf16[16,4,1,256]{3,0,2,1:T(8,128)(2,1)S(1)}, bf16[16,4,1,256]{3,0,2,1:T(8,128)(2,1)S(1)}, u32[]{:S(2)}, u32[]{:S(2)}) collective-permute-start(bf16[16,4,1,256]{3,0,2,1:T(8,128)(2,1)S(1)} %get-tuple-element.20), channel_id=1, source_target_pairs={{0,4},{4,8},{8,12},{1,5},{5,9},{9,13},{2,6},{6,10},{10,14},{3,7},{... | collective-permute-start | bytes 98312 | tf_op jit(solution)/shard_map/ppermute | solution.py:19
  122.1 3.5 %collective-permute-start.15 = (bf16[16,4,1,256]{3,0,2,1:T(8,128)(2,1)S(1)}, bf16[16,4,1,256]{3,0,2,1:T(8,128)(2,1)S(1)}, u32[]{:S(2)}, u32[]{:S(2)}) collective-permute-start(bf16[16,4,1,256]{3,0,2,1:T(8,128)(2,1)S(1)} %get-tuple-element.21), channel_id=1, source_target_pairs={{4,0},{8,4},{12,8},{5,1},{9,5},{13,9},{6,2},{10,6},{14,10},{7,3},{... | collective-permute-start | bytes 98312 | tf_op jit(solution)/shard_map/ppermute | solution.py:21
  125.7 4.5 %collective-permute-start.16 = (bf16[16,4,6,1]{3,0,2,1:T(8,128)(2,1)S(1)}, bf16[16,4,6,1]{3,0,2,1:T(8,128)(2,1)S(1)}, u32[]{:S(2)}, u32[]{:S(2)}) collective-permute-start(bf16[16,4,6,1]{3,0,2,1:T(8,128)(2,1)S(1)} %get-tuple-element.19), channel_id=1, source_target_pairs={{0,1},{1,2},{2,3},{4,5},{5,6},{6,7},{8,9},{9,10},{10,11},{12,13},{... | collective-permute-start | bytes 2312 | tf_op jit(solution)/shard_map/ppermute | solution.py:19
  128.1 6.5 %collective-permute-start.17 = (bf16[16,4,6,1]{3,0,2,1:T(8,128)(2,1)S(1)}, bf16[16,4,6,1]{3,0,2,1:T(8,128)(2,1)S(1)}, u32[]{:S(2)}, u32[]{:S(2)}) collective-permute-start(bf16[16,4,6,1]{3,0,2,1:T(8,128)(2,1)S(1)} %get-tuple-element.18), channel_id=1, source_target_pairs={{1,0},{2,1},{3,2},{5,4},{6,5},{7,6},{9,8},{10,9},{11,10},{13,12},{... | collective-permute-start | bytes 2312 | tf_op jit(solution)/shard_map/ppermute | solution.py:21
where the time goes:
time: 187 us; the launch traced here: 186 us
  blocking collectives  82.4 us (44%)
  starting transfers between devices  40 us (21%)
  waiting for transfers between devices  26.4 us (14%)
  other arithmetic  15.8 us (8%)
  matrix products  13.6 us (7%)
  local copies, waits for them, and re-layouts  6.08 us (3%)
    psum x1, blocking collectives, residual_gram(): return lax.psum(local_gram(residual, residual), ('gx', 'gy', 'gz'))  43.2 us
    psum x1, blocking collectives, on_device(): lax.psum((local_gram(direction, image), local_gram(image, residual), loca...  39.1 us
    ppermute x9, starting transfers between devices, padded_2(): lax.ppermute(tail, axis, [(i, (i + 1) % count) for i in range(ends)])  28.4 us
    ppermute x9, waiting for transfers between devices, padded_2(): lax.ppermute(head, axis, [((i + 1) % count, i) for i in range(ends)])  24.2 us
    ppermute x9, starting transfers between devices, padded_2(): lax.ppermute(head, axis, [((i + 1) % count, i) for i in range(ends)])  11.6 us
    dot_general x16, matrix products, apply_operator(): jnp.einsum('b,bcxyz->cxyz', kernel[corner], stacked, preferred_element_ty...  8.36 us
    another operation x9, other arithmetic, solve_small(): factor = jnp.linalg.cholesky(matrix)  6.4 us
    another operation x6, other arithmetic, solve_small(): return jax.scipy.linalg.cho_solve((factor, True), rhs_small)  5.63 us
  transfers between devices with their start and end apart: 18, of which 12 were waited for; matrix products, arithmetic and copies ran while one was open for 2% of the time, Pallas kernels for 0%

commit v1 on v0

--- a/solution.py
+++ b/solution.py
@@ -125,8 +125,15 @@
     for iteration in range(ITERS):
         image = apply_operator(direction, weights, kernel)
         curvature, cross, image_sq = lax.psum(
-            (local_gram(direction, image), local_gram(image, residual), local_gram(image, image)),
-            ("gx", "gy", "gz"),
+            lax.psum(
+                (
+                    local_gram(direction, image),
+                    local_gram(image, residual),
+                    local_gram(image, image),
+                ),
+                ("gy", "gz"),
+            ),
+            "gx",
         )
         alpha = solve_small(curvature, current)
         solution = solution + combine(direction, alpha)

time: 187 us -> 249 us (1.33)
  blocking collectives: 82.4 us -> 143 us
  waiting for transfers between devices: 26.4 us -> 29.9 us
    psum x1 -> x2, blocking collectives: 39.1 us -> 88.9 us  [on_device(): lax.psum((local_gram(direction, image), local_gram(image, residual), loca...]
    psum x0 -> x2, blocking collectives: none -> 12.5 us  [on_device(): lax.psum(lax.psum((local_gram(direction, image), local_gram(image, residu...]
    ppermute x9, waiting for transfers between devices: 24.2 us -> 27.8 us  [padded_2(): lax.ppermute(head, axis, [((i + 1) % count, i) for i in range(ends)])]
  transfers between devices with their start and end apart: 18 -> 18, of which waited for: 12 -> 11; matrix products, arithmetic and copies ran while one was open for 2% -> 3% of each run, Pallas kernels for 0% -> 0%
where the time goes in v1:
time: 249 us; the launch traced here: 248 us
  blocking collectives  143 us (57%)
  starting transfers between devices  38.5 us (15%)
  waiting for transfers between devices  29.9 us (12%)
  other arithmetic  15.8 us (6%)
  matrix products  13.6 us (5%)
  local copies, waits for them, and re-layouts  6.08 us (2%)
    psum x2, blocking collectives, on_device(): lax.psum((local_gram(direction, image), local_gram(image, residual), loca...  88.9 us
    psum x1, blocking collectives, residual_gram(): return lax.psum(local_gram(residual, residual), ('gx', 'gy', 'gz'))  41.7 us
    ppermute x9, waiting for transfers between devices, padded_2(): lax.ppermute(head, axis, [((i + 1) % count, i) for i in range(ends)])  27.8 us
    ppermute x9, starting transfers between devices, padded_2(): lax.ppermute(tail, axis, [(i, (i + 1) % count) for i in range(ends)])  26.9 us
    psum x2, blocking collectives, on_device(): lax.psum(lax.psum((local_gram(direction, image), local_gram(image, residu...  12.5 us
    ppermute x9, starting transfers between devices, padded_2(): lax.ppermute(head, axis, [((i + 1) % count, i) for i in range(ends)])  11.6 us
    dot_general x16, matrix products, apply_operator(): jnp.einsum('b,bcxyz->cxyz', kernel[corner], stacked, preferred_element_ty...  8.39 us
    another operation x9, other arithmetic, solve_small(): factor = jnp.linalg.cholesky(matrix)  6.39 us
  transfers between devices with their start and end apart: 18, of which 11 were waited for; matrix products, arithmetic and copies ran while one was open for 3% of the time, Pallas kernels for 0%

profile of v1, /device:TPU:0, one launch (start us, length us, event | category | flops | bytes accessed | tf_op | source)
XLA Modules:
  0.0 248.4 jit_solution(16700612459024689904)
XLA Ops:
  0.6 0.9 convert_element_type.9
  1.6 4.9 %collective-permute-start = (bf16[16,1,4,256]{3,2,1,0:T(4,128)(2,1)S(1)}, bf16[16,1,4,256]{3,2,1,0:T(4,128)(2,1)S(1)}, u32[]{:S(2)}, u32[]{:S(2)}) collective-permute-start(bf16[16,1,4,256]{3,2,1,0:T(4,128)(2,1)S(1)} %get-tuple-element.28), channel_id=1, source_target_pairs={{0,16},{1,17},{2,18},{3,19},{4,20},{5,21},{6,22},{7,23},{8,24},{9,... | collective-permute-start | bytes 98312 | tf_op jit(solution)/shard_map/ppermute | solution.py:19
  6.5 1.3 collective-permute-start.1
  7.8 0.8 select_reduce_fusion
  8.6 4.5 %collective-permute-start.6 = (f32[1,4,256]{2,1,0:T(4,128)S(1)}, f32[1,4,256]{2,1,0:T(4,128)S(1)}, u32[]{:S(2)}, u32[]{:S(2)}) collective-permute-start(f32[1,4,256]{2,1,0:T(4,128)S(1)} %get-tuple-element.44), channel_id=1, source_target_pairs={{0,16},{1,17},{2,18},{3,19},{4,20},{5,21},{6,22},{7,23},{8,24},{9,... | collective-permute-start | bytes 12296 | tf_op jit(solution)/shard_map/ppermute | solution.py:19
  13.2 1.3 collective-permute-start.7
  14.5 1.3 convolution_bitcast_fusion.4
  15.7 41.7 %psum.65 = f32[16,16]{0,1:T(8,128)S(1)} all-reduce(f32[16,16]{0,1:T(8,128)S(1)} %convolution_bitcast_fusion.4), channel_id=1, replica_groups=mesh['gx'=2,'gy'=4,'gz'=4] {'gx','gy','gz'}, use_global_device_ids=true, to_apply=%region_5.0 | all-reduce | flops 256 | bytes 2048 | tf_op jit(solution)/shard_map/psum | solution.py:102
  57.5 1.5 cholesky.70
  59.0 0.6 compare_reduce_fusion.1
  59.7 1.3 collective-permute-start.8
  60.9 1.3 collective-permute-start.9
  62.2 0.7 fusion.56
  62.9 1.2 custom-call.10
  64.1 2.4 collective-permute-done.9
  66.6 3.4 %collective-permute-start.10 = (f32[4,6,1]{2,1,0:T(8,128)S(1)}, f32[4,6,1]{2,1,0:T(8,128)S(1)}, u32[]{:S(2)}, u32[]{:S(2)}) collective-permute-start(f32[4,6,1]{2,1,0:T(8,128)S(1)} %get-tuple-element.38), channel_id=1, source_target_pairs={{0,1},{1,2},{2,3},{4,5},{5,6},{6,7},{8,9},{9,10},{10,11},{12,13},{... | collective-permute-start | bytes 296 | tf_op jit(solution)/shard_map/ppermute | solution.py:19
  70.0 1.3 collective-permute-start.11
  71.4 4.2 %collective-permute-done.11 = f32[4,6,1]{2,1,0:T(8,128)S(1)} collective-permute-done((f32[4,6,1]{2,1,0:T(8,128)S(1)}, f32[4,6,1]{2,1,0:T(8,128)S(1)}, u32[]{:S(2)}, u32[]{:S(2)}) %collective-permute-start.11) | collective-permute-done | bytes 128 | tf_op jit(solution)/shard_map/ppermute | solution.py:21
  76.0 2.8 %collective-permute-start.2 = (bf16[16,4,1,256]{3,2,1,0:T(2,128)(2,1)S(1)}, bf16[16,4,1,256]{3,2,1,0:T(2,128)(2,1)S(1)}, u32[]{:S(2)}, u32[]{:S(2)}) collective-permute-start(bf16[16,4,1,256]{3,2,1,0:T(2,128)(2,1)S(1)} %get-tuple-element.24), channel_id=1, source_target_pairs={{0,4},{4,8},{8,12},{1,5},{5,9},{9,13},{2,6},{6,10},{10,14},{3,7},{... | collective-permute-start | bytes 98312 | tf_op jit(solution)/shard_map/ppermute | solution.py:19
  78.8 1.3 collective-permute-start.3
  80.2 3.4 %collective-permute-done.3 = bf16[16,4,1,256]{3,2,1,0:T(2,128)(2,1)S(1)} collective-permute-done((bf16[16,4,1,256]{3,2,1,0:T(2,128)(2,1)S(1)}, bf16[16,4,1,256]{3,2,1,0:T(2,128)(2,1)S(1)}, u32[]{:S(2)}, u32[]{:S(2)}) %collective-permute-start.3) | collective-permute-done | bytes 32800 | tf_op jit(solution)/shard_map/ppermute | solution.py:21
  83.9 3.3 %collective-permute-start.4 = (bf16[16,4,6,1]{3,2,1,0:T(8,128)(2,1)S(1)}, bf16[16,4,6,1]{3,2,1,0:T(8,128)(2,1)S(1)}, u32[]{:S(2)}, u32[]{:S(2)}) collective-permute-start(bf16[16,4,6,1]{3,2,1,0:T(8,128)(2,1)S(1)} %get-tuple-element.17), channel_id=1, source_target_pairs={{0,1},{1,2},{2,3},{4,5},{5,6},{6,7},{8,9},{9,10},{10,11},{12,13},{... | collective-permute-start | bytes 2312 | tf_op jit(solution)/shard_map/ppermute | solution.py:19
  87.2 1.3 collective-permute-start.5
  88.6 1.1 collective-permute-done.4
  89.7 4.4 %collective-permute-done.5 = bf16[16,4,6,1]{3,2,1,0:T(8,128)(2,1)S(1)} collective-permute-done((bf16[16,4,6,1]{3,2,1,0:T(8,128)(2,1)S(1)}, bf16[16,4,6,1]{3,2,1,0:T(8,128)(2,1)S(1)}, u32[]{:S(2)}, u32[]{:S(2)}) %collective-permute-start.5) | collective-permute-done | bytes 800 | tf_op jit(solution)/shard_map/ppermute | solution.py:21
  94.1 0.9 pad_maximum_fusion
  95.5 1.6 copy.46
  97.2 0.5 fusion.82
  97.8 0.5 fusion.83
  98.4 0.5 fusion.84
  99.0 0.5 fusion.85
  99.5 0.5 fusion.86
  100.1 0.5 fusion.87
  100.6 0.5 fusion.88
  101.1 0.5 fusion.89
  102.0 0.8 copy-done
  103.5 58.3 %all-reduce = (f32[16,16]{0,1:T(8,128)S(1)}, f32[16,16]{1,0:T(8,128)S(1)}, f32[16,16]{1,0:T(8,128)S(1)}) all-reduce(f32[16,16]{0,1:T(8,128)S(1)} %bitcast.265, f32[16,16]{1,0:T(8,128)S(1)} %convolution_bitcast_fusion.3, f32[16,16]{1,0:T(8,128)S(1)} %bitcast.266), channel_id=1, replica_groups=mesh['gx'=2,'gy'=4,'gz'=4] {'gy','gz'}, use_global_device_ids=true, to_apply=%region_1.2 | all-reduce | flops 768 | bytes 6144 | tf_op jit(solution)/shard_map/psum | solution.py:128
  161.8 7.5 %all-reduce.1 = (f32[16,16]{0,1:T(8,128)S(1)}, f32[16,16]{1,0:T(8,128)S(1)}, f32[16,16]{1,0:T(8,128)S(1)}) all-reduce(f32[16,16]{0,1:T(8,128)S(1)} %get-tuple-element.8, f32[16,16]{1,0:T(8,128)S(1)} %get-tuple-element.9, f32[16,16]{1,0:T(8,128)S(1)} %get-tuple-element.10), channel_id=1, replica_groups=mesh['gx'=2,'gy'=4,'gz'=4] {'gx'}, use_global_device_ids=true, to_apply=%region_2.3 | all-reduce | flops 768 | bytes 6144 | tf_op jit(solution)/shard_map/psum | solution.py:127
  169.4 1.5 cholesky.59
  170.9 0.6 compare_reduce_fusion.2
  171.5 0.6 fusion.55
  172.2 1.2 custom-call.9
  175.5 3.4 %collective-permute-start.12 = (bf16[16,1,4,256]{3,0,2,1:T(8,128)(2,1)S(1)}, bf16[16,1,4,256]{3,0,2,1:T(8,128)(2,1)S(1)}, u32[]{:S(2)}, u32[]{:S(2)}) collective-permute-start(bf16[16,1,4,256]{3,0,2,1:T(8,128)(2,1)S(1)} %get-tuple-element.26), channel_id=1, source_target_pairs={{0,16},{1,17},{2,18},{3,19},{4,20},{5,21},{6,22},{7,23},{8,24},{9,... | collective-permute-start | bytes 98312 | tf_op jit(solution)/shard_map/ppermute | solution.py:19
  178.9 1.3 collective-permute-start.13
  180.5 4.2 %collective-permute-done.13 = bf16[16,1,4,256]{3,0,2,1:T(8,128)(2,1)S(1)} collective-permute-done((bf16[16,1,4,256]{3,0,2,1:T(8,128)(2,1)S(1)}, bf16[16,1,4,256]{3,0,2,1:T(8,128)(2,1)S(1)}, u32[]{:S(2)}, u32[]{:S(2)}) %collective-permute-start.13) | collective-permute-done | bytes 32800 | tf_op jit(solution)/shard_map/ppermute | solution.py:21
  184.7 1.3 collective-permute-start.14
  186.0 1.3 collective-permute-start.15
  187.3 4.9 %collective-permute-done.15 = bf16[16,4,1,256]{3,0,2,1:T(8,128)(2,1)S(1)} collective-permute-done((bf16[16,4,1,256]{3,0,2,1:T(8,128)(2,1)S(1)}, bf16[16,4,1,256]{3,0,2,1:T(8,128)(2,1)S(1)}, u32[]{:S(2)}, u32[]{:S(2)}) %collective-permute-start.15) | collective-permute-done | bytes 32800 | tf_op jit(solution)/shard_map/ppermute | solution.py:21
  192.3 1.9 collective-permute-start.16
  194.2 1.3 collective-permute-start.17
  195.9 0.6 collective-permute-done.16
  196.4 4.3 %collective-permute-done.17 = bf16[16,4,6,1]{3,0,2,1:T(8,128)(2,1)S(1)} collective-permute-done((bf16[16,4,6,1]{3,0,2,1:T(8,128)(2,1)S(1)}, bf16[16,4,6,1]{3,0,2,1:T(8,128)(2,1)S(1)}, u32[]{:S(2)}, u32[]{:S(2)}) %collective-permute-start.17) | collective-permute-done | bytes 800 | tf_op jit(solution)/shard_map/ppermute | solution.py:21
  202.3 0.5 fusion.12
  202.8 0.5 fusion.14
  203.9 0.5 fusion.18
  204.4 0.5 fusion.20
  206.2 30.6 %psum.70 = f32[16,16]{0,1:T(8,128)S(1)} all-reduce(f32[16,16]{0,1:T(8,128)S(1)} %convolution_bitcast_fusion.1), channel_id=1, replica_groups=mesh['gx'=2,'gy'=4,'gz'=4] {'gy','gz'}, use_global_device_ids=true, to_apply=%region_10.13 | all-reduce | flops 256 | bytes 2048 | tf_op jit(solution)/shard_map/psum | solution.py:128
  236.9 5.0 %psum.71 = f32[16,16]{0,1:T(8,128)S(1)} all-reduce(f32[16,16]{0,1:T(8,128)S(1)} %psum.70), channel_id=1, replica_groups=mesh['gx'=2,'gy'=4,'gz'=4] {'gx'}, use_global_device_ids=true, to_apply=%region_11.14 | all-reduce | flops 256 | bytes 2048 | tf_op jit(solution)/shard_map/psum | solution.py:127
  242.0 1.5 cholesky.81
  243.4 0.6 compare_reduce_fusion
  244.1 0.6 fusion.57
  244.7 1.2 custom-call.11
  246.7 0.7 copy.45
  247.7 0.7 copy.44
  (104 shorter events, 10.0 us)
Async XLA Ops:
  1.6 74.2 %collective-permute-start = (bf16[16,1,4,256]{3,2,1,0:T(4,128)(2,1)S(1)}, bf16[16,1,4,256]{3,2,1,0:T(4,128)(2,1)S(1)}, u32[]{:S(2)}, u32[]{:S(2)}) collective-permute-start(bf16[16,1,4,256]{3,2,1,0:T(4,128)(2,1)S(1)} %get-tuple-element.28), channel_id=1, source_target_pairs={{0,16},{1,17},{2,18},{3,19},{4,20},{5,21},{6,22},{7,23},{8,24},{9,... | collective-permute-start | bytes 98312 | tf_op jit(solution)/shard_map/ppermute | solution.py:19
  6.5 69.3 %collective-permute-start.1 = (bf16[16,1,4,256]{3,2,1,0:T(4,128)(2,1)S(1)}, bf16[16,1,4,256]{3,2,1,0:T(4,128)(2,1)S(1)}, u32[]{:S(2)}, u32[]{:S(2)}) collective-permute-start(bf16[16,1,4,256]{3,2,1,0:T(4,128)(2,1)S(1)} %get-tuple-element.29), channel_id=1, source_target_pairs={{16,0},{17,1},{18,2},{19,3},{20,4},{21,5},{22,6},{23,7},{24,8},{25... | collective-permute-start | bytes 98312 | tf_op jit(solution)/shard_map/ppermute | solution.py:21
  8.6 51.0 %collective-permute-start.6 = (f32[1,4,256]{2,1,0:T(4,128)S(1)}, f32[1,4,256]{2,1,0:T(4,128)S(1)}, u32[]{:S(2)}, u32[]{:S(2)}) collective-permute-start(f32[1,4,256]{2,1,0:T(4,128)S(1)} %get-tuple-element.44), channel_id=1, source_target_pairs={{0,16},{1,17},{2,18},{3,19},{4,20},{5,21},{6,22},{7,23},{8,24},{9,... | collective-permute-start | bytes 12296 | tf_op jit(solution)/shard_map/ppermute | solution.py:19
  13.2 46.5 %collective-permute-start.7 = (f32[1,4,256]{2,1,0:T(4,128)S(1)}, f32[1,4,256]{2,1,0:T(4,128)S(1)}, u32[]{:S(2)}, u32[]{:S(2)}) collective-permute-start(f32[1,4,256]{2,1,0:T(4,128)S(1)} %get-tuple-element.45), channel_id=1, source_target_pairs={{16,0},{17,1},{18,2},{19,3},{20,4},{21,5},{22,6},{23,7},{24,8},{25... | collective-permute-start | bytes 12296 | tf_op jit(solution)/shard_map/ppermute | solution.py:21
  59.7 4.5 %collective-permute-start.8 = (f32[4,1,256]{2,1,0:T(1,128)S(1)}, f32[4,1,256]{2,1,0:T(1,128)S(1)}, u32[]{:S(2)}, u32[]{:S(2)}) collective-permute-start(f32[4,1,256]{2,1,0:T(1,128)S(1)} %get-tuple-element.42), channel_id=1, source_target_pairs={{0,4},{4,8},{8,12},{1,5},{5,9},{9,13},{2,6},{6,10},{10,14},{3,7},{... | collective-permute-start | bytes 12296 | tf_op jit(solution)/shard_map/ppermute | solution.py:19
  60.9 5.6 %collective-permute-start.9 = (f32[4,1,256]{2,1,0:T(1,128)S(1)}, f32[4,1,256]{2,1,0:T(1,128)S(1)}, u32[]{:S(2)}, u32[]{:S(2)}) collective-permute-start(f32[4,1,256]{2,1,0:T(1,128)S(1)} %get-tuple-element.43), channel_id=1, source_target_pairs={{4,0},{8,4},{12,8},{5,1},{9,5},{13,9},{6,2},{10,6},{14,10},{7,3},{... | collective-permute-start | bytes 12296 | tf_op jit(solution)/shard_map/ppermute | solution.py:21
  66.6 4.8 %collective-permute-start.10 = (f32[4,6,1]{2,1,0:T(8,128)S(1)}, f32[4,6,1]{2,1,0:T(8,128)S(1)}, u32[]{:S(2)}, u32[]{:S(2)}) collective-permute-start(f32[4,6,1]{2,1,0:T(8,128)S(1)} %get-tuple-element.38), channel_id=1, source_target_pairs={{0,1},{1,2},{2,3},{4,5},{5,6},{6,7},{8,9},{9,10},{10,11},{12,13},{... | collective-permute-start | bytes 296 | tf_op jit(solution)/shard_map/ppermute | solution.py:19
  70.0 5.6 %collective-permute-start.11 = (f32[4,6,1]{2,1,0:T(8,128)S(1)}, f32[4,6,1]{2,1,0:T(8,128)S(1)}, u32[]{:S(2)}, u32[]{:S(2)}) collective-permute-start(f32[4,6,1]{2,1,0:T(8,128)S(1)} %get-tuple-element.39), channel_id=1, source_target_pairs={{1,0},{2,1},{3,2},{5,4},{6,5},{7,6},{9,8},{10,9},{11,10},{13,12},{... | collective-permute-start | bytes 296 | tf_op jit(solution)/shard_map/ppermute | solution.py:21
  76.0 4.2 %collective-permute-start.2 = (bf16[16,4,1,256]{3,2,1,0:T(2,128)(2,1)S(1)}, bf16[16,4,1,256]{3,2,1,0:T(2,128)(2,1)S(1)}, u32[]{:S(2)}, u32[]{:S(2)}) collective-permute-start(bf16[16,4,1,256]{3,2,1,0:T(2,128)(2,1)S(1)} %get-tuple-element.24), channel_id=1, source_target_pairs={{0,4},{4,8},{8,12},{1,5},{5,9},{9,13},{2,6},{6,10},{10,14},{3,7},{... | collective-permute-start | bytes 98312 | tf_op jit(solution)/shard_map/ppermute | solution.py:19
  78.8 4.7 %collective-permute-start.3 = (bf16[16,4,1,256]{3,2,1,0:T(2,128)(2,1)S(1)}, bf16[16,4,1,256]{3,2,1,0:T(2,128)(2,1)S(1)}, u32[]{:S(2)}, u32[]{:S(2)}) collective-permute-start(bf16[16,4,1,256]{3,2,1,0:T(2,128)(2,1)S(1)} %get-tuple-element.25), channel_id=1, source_target_pairs={{4,0},{8,4},{12,8},{5,1},{9,5},{13,9},{6,2},{10,6},{14,10},{7,3},{... | collective-permute-start | bytes 98312 | tf_op jit(solution)/shard_map/ppermute | solution.py:21
  83.9 5.8 %collective-permute-start.4 = (bf16[16,4,6,1]{3,2,1,0:T(8,128)(2,1)S(1)}, bf16[16,4,6,1]{3,2,1,0:T(8,128)(2,1)S(1)}, u32[]{:S(2)}, u32[]{:S(2)}) collective-permute-start(bf16[16,4,6,1]{3,2,1,0:T(8,128)(2,1)S(1)} %get-tuple-element.17), channel_id=1, source_target_pairs={{0,1},{1,2},{2,3},{4,5},{5,6},{6,7},{8,9},{9,10},{10,11},{12,13},{... | collective-permute-start | bytes 2312 | tf_op jit(solution)/shard_map/ppermute | solution.py:19
  87.2 6.9 %collective-permute-start.5 = (bf16[16,4,6,1]{3,2,1,0:T(8,128)(2,1)S(1)}, bf16[16,4,6,1]{3,2,1,0:T(8,128)(2,1)S(1)}, u32[]{:S(2)}, u32[]{:S(2)}) collective-permute-start(bf16[16,4,6,1]{3,2,1,0:T(8,128)(2,1)S(1)} %get-tuple-element.16), channel_id=1, source_target_pairs={{1,0},{2,1},{3,2},{5,4},{6,5},{7,6},{9,8},{10,9},{11,10},{13,12},{... | collective-permute-start | bytes 2312 | tf_op jit(solution)/shard_map/ppermute | solution.py:21
  95.5 1.6 copy-start.1
  97.2 0.7 copy-start.2
  97.2 1.2 copy-start.3
  97.8 1.1 copy-start.4
  98.4 1.1 copy-start.5
  98.9 1.1 copy-start.6
  99.5 1.1 copy-start.7
  100.1 1.1 copy-start.8
  101.8 0.9 copy-start
  175.5 5.0 %collective-permute-start.12 = (bf16[16,1,4,256]{3,0,2,1:T(8,128)(2,1)S(1)}, bf16[16,1,4,256]{3,0,2,1:T(8,128)(2,1)S(1)}, u32[]{:S(2)}, u32[]{:S(2)}) collective-permute-start(bf16[16,1,4,256]{3,0,2,1:T(8,128)(2,1)S(1)} %get-tuple-element.26), channel_id=1, source_target_pairs={{0,16},{1,17},{2,18},{3,19},{4,20},{5,21},{6,22},{7,23},{8,24},{9,... | collective-permute-start | bytes 98312 | tf_op jit(solution)/shard_map/ppermute | solution.py:19
  178.9 5.8 %collective-permute-start.13 = (bf16[16,1,4,256]{3,0,2,1:T(8,128)(2,1)S(1)}, bf16[16,1,4,256]{3,0,2,1:T(8,128)(2,1)S(1)}, u32[]{:S(2)}, u32[]{:S(2)}) collective-permute-start(bf16[16,1,4,256]{3,0,2,1:T(8,128)(2,1)S(1)} %get-tuple-element.27), channel_id=1, source_target_pairs={{16,0},{17,1},{18,2},{19,3},{20,4},{21,5},{22,6},{23,7},{24,8},{25... | collective-permute-start | bytes 98312 | tf_op jit(solution)/shard_map/ppermute | solution.py:21
  184.7 2.6 %collective-permute-start.14 = (bf16[16,4,1,256]{3,0,2,1:T(8,128)(2,1)S(1)}, bf16[16,4,1,256]{3,0,2,1:T(8,128)(2,1)S(1)}, u32[]{:S(2)}, u32[]{:S(2)}) collective-permute-start(bf16[16,4,1,256]{3,0,2,1:T(8,128)(2,1)S(1)} %get-tuple-element.22), channel_id=1, source_target_pairs={{0,4},{4,8},{8,12},{1,5},{5,9},{9,13},{2,6},{6,10},{10,14},{3,7},{... | collective-permute-start | bytes 98312 | tf_op jit(solution)/shard_map/ppermute | solution.py:19
  186.0 6.2 %collective-permute-start.15 = (bf16[16,4,1,256]{3,0,2,1:T(8,128)(2,1)S(1)}, bf16[16,4,1,256]{3,0,2,1:T(8,128)(2,1)S(1)}, u32[]{:S(2)}, u32[]{:S(2)}) collective-permute-start(bf16[16,4,1,256]{3,0,2,1:T(8,128)(2,1)S(1)} %get-tuple-element.23), channel_id=1, source_target_pairs={{4,0},{8,4},{12,8},{5,1},{9,5},{13,9},{6,2},{10,6},{14,10},{7,3},{... | collective-permute-start | bytes 98312 | tf_op jit(solution)/shard_map/ppermute | solution.py:21
  192.3 4.1 %collective-permute-start.16 = (bf16[16,4,6,1]{3,0,2,1:T(8,128)(2,1)S(1)}, bf16[16,4,6,1]{3,0,2,1:T(8,128)(2,1)S(1)}, u32[]{:S(2)}, u32[]{:S(2)}) collective-permute-start(bf16[16,4,6,1]{3,0,2,1:T(8,128)(2,1)S(1)} %get-tuple-element.21), channel_id=1, source_target_pairs={{0,1},{1,2},{2,3},{4,5},{5,6},{6,7},{8,9},{9,10},{10,11},{12,13},{... | collective-permute-start | bytes 2312 | tf_op jit(solution)/shard_map/ppermute | solution.py:19
  194.2 6.5 %collective-permute-start.17 = (bf16[16,4,6,1]{3,0,2,1:T(8,128)(2,1)S(1)}, bf16[16,4,6,1]{3,0,2,1:T(8,128)(2,1)S(1)}, u32[]{:S(2)}, u32[]{:S(2)}) collective-permute-start(bf16[16,4,6,1]{3,0,2,1:T(8,128)(2,1)S(1)} %get-tuple-element.20), channel_id=1, source_target_pairs={{1,0},{2,1},{3,2},{5,4},{6,5},{7,6},{9,8},{10,9},{11,10},{13,12},{... | collective-permute-start | bytes 2312 | tf_op jit(solution)/shard_map/ppermute | solution.py:21
